TPU v7x, 256 devices: a whole 4x4x8 slice. The times are simulated.
256 devices in a mesh: tp: 4 (over x), dp: 64 (over z, y, core).
Axes of the slice: x: 4, y: 4, z: 8, core: 2. Of those that a mesh axis runs over, the one named last changes fastest.
Arguments:
- g_qkv: bfloat16 [64, 512, 16, 3, 64], P('dp', None, 'tp')
- g_out: bfloat16 [64, 1024, 512], P('dp', 'tp')
- g_up: bfloat16 [64, 512, 2048], P('dp', None, 'tp')
- g_down: bfloat16 [64, 2048, 512], P('dp', 'tp')
- g_norms: bfloat16 [64, 6, 512], P('dp')
- master: float32 [4, 1051648], P('tp', 'dp')
- mom_one: float32 [4, 1051648], P('tp', 'dp')
- mom_two: float32 [4, 1051648], P('tp', 'dp')
Outputs:
- output 1: bfloat16 [512, 16, 3, 64], P(None, 'tp')
- output 2: bfloat16 [1024, 512], P('tp')
- output 3: bfloat16 [512, 2048], P(None, 'tp')
- output 4: bfloat16 [2048, 512], P('tp')
- output 5: bfloat16 [6, 512], replicated
- output 6: float32 [4, 1051648], P('tp', 'dp')
- output 7: float32 [4, 1051648], P('tp', 'dp')
- output 8: float32 [4, 1051648], P('tp', 'dp')
- output 9: float32 [], replicated
All inputs are finite; a program needn't handle non-finite values.
Results may differ from a plain program's by a relative error of at most 0.001.
Values are sent between devices in bfloat16 or wider.
A program may use at most 768 MiB of HBM per device.

v0:
```python
import math
import jax
import jax.numpy as jnp
from jax import lax
from jax.sharding import PartitionSpec as P

STEP = 20
BETA_ONE = 0.9
BETA_TWO = 0.95
ADAM_EPS = 1e-8
DECAY = 0.1
LEARN_RATE = 1e-4
MAX_NORM = 1.0
NORM_EPS = 1e-6
BIAS_ONE = 1.0 - BETA_ONE ** STEP
BIAS_TWO = 1.0 - BETA_TWO ** STEP
ARG_SPECS = (P("dp", None, "tp", None, None), P("dp", "tp", None), P("dp", None, "tp"), P("dp", "tp", None), P("dp", None, None), P("tp", "dp"), P("tp", "dp"), P("tp", "dp"))
OUT_SPECS = (P(None, "tp", None, None), P("tp", None), P(None, "tp"), P("tp", None), P(None, None), P("tp", "dp"), P("tp", "dp"), P("tp", "dp"), P())


def adamw_update(grad_clip, master, mom_one, mom_two, is_matrix):
    m_new = BETA_ONE * mom_one + (1.0 - BETA_ONE) * grad_clip
    v_new = BETA_TWO * mom_two + (1.0 - BETA_TWO) * grad_clip * grad_clip
    step_dir = (m_new / BIAS_ONE) / (jnp.sqrt(v_new / BIAS_TWO) + ADAM_EPS)
    master_new = master - LEARN_RATE * (step_dir + jnp.where(is_matrix, DECAY * master, 0.0))
    return master_new, m_new, v_new


def split_params(param_flat, shapes):
    pieces = []
    offset = 0
    for shape in shapes:
        elem_count = math.prod(shape)
        pieces.append(param_flat[offset:offset + elem_count].reshape(shape))
        offset += elem_count
    return tuple(pieces)


def solution(mesh):
    dp_size = mesh.shape["dp"]

    def local_step(g_qkv, g_out, g_up, g_down, g_norms, master, mom_one, mom_two):
        grads = (g_qkv, g_out, g_up, g_down, g_norms)
        shapes = [grad.shape[1:] for grad in grads]
        flat_grad = jnp.concatenate([grad.reshape(-1) for grad in grads])
        flat_count = flat_grad.shape[0]
        mat_count = flat_count - g_norms.size
        part_len = flat_count // dp_size
        received = lax.all_to_all(flat_grad.reshape(dp_size, part_len), "dp", 0, 0, tiled=True)
        grad_mean = jnp.sum(received, axis=0, dtype=jnp.float32) / dp_size
        flat_index = lax.axis_index("dp") * part_len + jnp.arange(part_len)
        is_matrix = flat_index < mat_count
        counted = jnp.logical_or(is_matrix, lax.axis_index("tp") == 0)
        local_sq = jnp.sum(jnp.where(counted, grad_mean * grad_mean, 0.0))
        grad_norm = jnp.sqrt(lax.psum(local_sq, ("tp", "dp")))
        clip = jnp.minimum(1.0, MAX_NORM / (grad_norm + NORM_EPS))
        master_new, m_new, v_new = adamw_update(grad_mean * clip, master[0], mom_one[0], mom_two[0], is_matrix)
        param_flat = lax.all_gather(master_new.astype(jnp.bfloat16), "dp", axis=0, tiled=True)
        params = split_params(param_flat, shapes)
        return params + (master_new[None], m_new[None], v_new[None], grad_norm)

    return jax.shard_map(local_step, mesh=mesh, in_specs=ARG_SPECS, out_specs=OUT_SPECS, check_vma=False)
```

profile of v0, /device:TPU:1, one launch (start us, length us, event | category | flops | bytes accessed | tf_op | source)
XLA Modules:
  0.0 393.3 jit_solution(11555953914343188922)
XLA Ops:
  7.2 3.2 copy.19
  10.4 0.0 copy-start.6
  10.4 1.1 reshape.114
  11.5 0.0 copy-start.1
  11.5 0.0 copy-start.2
  11.5 0.0 copy-start.7
  11.5 0.1 constant_dynamic-update-slice_fusion.4
  11.6 0.0 copy-done.6
  11.6 0.1 copy.22
  11.7 0.8 copy-done.1
  12.5 0.2 copy.23
  12.7 0.0 copy-done.2
  12.8 0.2 copy.24
  13.0 0.0 copy-done.7
  13.1 4.0 %all_to_all.8 = bf16[64,1,16432]{2,1,0:T(2,128)(2,1)} reshape(bf16[1051648]{0:T(1024)(128)(2,1)S(1)} %constant_dynamic-update-slice_fusion) | data formatting | bytes 4206592 | tf_op jit(solution)/shard_map/all_to_all | solution.py:49
  17.1 0.5 broadcast.77
  17.6 13.5 %reduce.6 = bf16[64,16432]{1,0:T(8,128)(2,1)S(1)} reduce(bf16[64,1,16432]{2,1,0:T(2,128)(2,1)} %all_to_all.8, bf16[]{:T(256)} %broadcast.77), dimensions={1}, to_apply=%all_to_all.8.reduce_sub_computation | reduce | bytes 4206594 | tf_op jit(solution)/shard_map/all_to_all | solution.py:49
  31.2 2.8 reshape.128
  34.0 0.0 copy-start.3
  34.0 0.0 copy-start.8
  34.0 0.0 copy-start.4
  34.0 0.0 copy-start.5
  34.0 13.3 %all-to-all-start = ((bf16[64,2,8216]{2,1,0:T(2,128)(2,1)}), bf16[64,2,8216]{2,1,0:T(2,128)(2,1)S(1)}, u32[]{:S(2)}, u32[]{:S(2)}) async-start(bf16[64,2,8216]{2,1,0:T(2,128)(2,1)} %reshape.128), calls=%async_computation | async-start | bytes 4259840 | tf_op jit(solution)/shard_map/all_to_all | solution.py:49
  47.3 0.2 all-reduce.3.cloned.1.call-start
  47.6 0.0 copy-done.3
  47.6 0.2 reduce.1
  47.8 0.0 copy-done.8
  47.8 0.6 dynamic-slice
  48.4 0.0 copy-done.4
  48.4 0.0 copy-done.5
  48.4 0.4 multiply_reduce_fusion
  48.8 48.9 %all-to-all-done = bf16[64,2,8216]{2,1,0:T(2,128)(2,1)S(1)} async-done(((bf16[64,2,8216]{2,1,0:T(2,128)(2,1)}), bf16[64,2,8216]{2,1,0:T(2,128)(2,1)S(1)}, u32[]{:S(2)}, u32[]{:S(2)}) %all-to-all-start) | async-done | bytes 2103328 | tf_op jit(solution)/shard_map/all_to_all | solution.py:49
  97.6 7.1 %reshape.129 = bf16[64,1,16432]{2,1,0:T(2,128)(2,1)} reshape(bf16[64,2,8216]{2,1,0:T(2,128)(2,1)S(1)} %all-to-all-done) | data formatting | bytes 4206592
  104.7 6.6 %convert_reduce_fusion = f32[16432]{0:T(1024)S(1)} fusion(bf16[64,1,16432]{2,1,0:T(2,128)(2,1)} %reshape.129), kind=kLoop, calls=%fused_computation | loop fusion | flops 2086864 | bytes 2169024 | tf_op jit(solution)/shard_map/reduce_sum | solution.py:50
  111.3 0.6 select_reduce_fusion
  112.6 77.7 %psum.7 = f32[]{:T(128)} all-reduce(f32[]{:T(128)} %select_reduce_fusion), channel_id=1, replica_groups=mesh['tp'=4,'dp'=64] {'tp','dp'}, use_global_device_ids=true, to_apply=%region_2.3 | all-reduce | flops 1 | bytes 8 | tf_op jit(solution)/shard_map/psum | solution.py:55
  191.1 0.1 subtract_convert_fusion
  191.1 0.2 broadcast.69
  191.3 0.6 dynamic-update-slice
  191.9 0.0 copy-start
  191.9 1.3 copy-done
  193.2 0.0 all-reduce.3.cloned.1.call-update
  193.3 1.2 multiply_subtract_fusion
  194.4 182.2 %all-reduce.3.cloned.1.call-done = bf16[1051648]{0:T(1024)(128)(2,1)} async-done(((bf16[1051648]{0:T(1024)(128)(2,1)}), bf16[1051648]{0:T(1024)(128)(2,1)}) %all-reduce.3.cloned.1.call-update) | async-done | bytes 2103312
  376.6 1.3 fusion.10
  377.9 0.0 slice-start
  377.9 1.1 slice.59
  379.0 1.1 slice.61
  380.1 0.0 slice-done
  380.1 1.1 reshape.119
  381.2 0.0 slice-start.1
  381.2 0.0 slice-start.2
  381.3 2.6 copy.21
  383.9 0.0 slice-done.1
  383.9 0.9 slice.57
  384.7 0.0 slice-done.2
  384.7 0.6 slice.63
  (5 shorter events, 0.1 us)
Async XLA Ops:
  10.4 1.2 copy-start.6
  11.5 1.0 copy-start.1
  11.5 1.2 copy-start.2
  11.5 1.5 copy-start.7
  34.0 13.6 %copy-start.3 = (f32[1,16432]{1,0:T(1,128)S(1)}, f32[1,16432]{1,0:T(1,128)}, u32[]{:S(2)}) copy-start(f32[1,16432]{1,0:T(1,128)} %param.13) | copy-start | bytes 197188
  34.0 13.7 %copy-start.8 = (u32[256]{0:T(256)S(1)}, u32[256]{0:T(256)}, u32[]{:S(2)}) copy-start(u32[256]{0:T(256)} %constant.52) | copy-start | bytes 3076
  34.0 14.3 %copy-start.4 = (f32[1,16432]{1,0:T(1,128)S(1)}, f32[1,16432]{1,0:T(1,128)}, u32[]{:S(2)}) copy-start(f32[1,16432]{1,0:T(1,128)} %param.15) | copy-start | bytes 197188
  34.0 14.3 %copy-start.5 = (f32[1,16432]{1,0:T(1,128)S(1)}, f32[1,16432]{1,0:T(1,128)}, u32[]{:S(2)}) copy-start(f32[1,16432]{1,0:T(1,128)} %param.14) | copy-start | bytes 197188
  34.0 63.6 %all-to-all-start = ((bf16[64,2,8216]{2,1,0:T(2,128)(2,1)}), bf16[64,2,8216]{2,1,0:T(2,128)(2,1)S(1)}, u32[]{:S(2)}, u32[]{:S(2)}) async-start(bf16[64,2,8216]{2,1,0:T(2,128)(2,1)} %reshape.128), calls=%async_computation | async-start | bytes 4259840 | tf_op jit(solution)/shard_map/all_to_all | solution.py:49
  47.3 329.3 %all-reduce.3.cloned.1.call-start = ((), (), s32[]{:S(2)}) async-start(), calls=%async_computation.1 | async-start | bytes 4206592
  191.9 1.3 copy-start
  377.9 2.2 slice-start
  381.2 2.6 slice-start.1
  381.2 3.5 slice-start.2
Sparse Core Ops, SparseCore 0:
  193.4 183.1 all-reduce.2
where the time goes:
time: 395 us; the launch traced here: 393 us
  waiting for transfers between devices  231 us (58%)
  blocking collectives  77.7 us (20%)
  local copies, waits for them, and re-layouts  31.6 us (8%)
  other arithmetic  22.6 us (6%)
  between operations  16.8 us (4%)
  starting transfers between devices  13.5 us (3%)
    unnamed x2, waiting for transfers between devices  182 us
    psum x1, blocking collectives, local_step(): grad_norm = jnp.sqrt(lax.psum(local_sq, ('tp', 'dp')))  77.7 us
    all_to_all x1, waiting for transfers between devices, local_step(): lax.all_to_all(flat_grad.reshape(dp_size, part_len), 'dp', 0, 0, tiled=True)  48.9 us
    unnamed x32, local copies, waits for them, and re-layouts  19.9 us
    all_to_all x1, other arithmetic, local_step(): lax.all_to_all(flat_grad.reshape(dp_size, part_len), 'dp', 0, 0, tiled=True)  13.5 us
    all_to_all x1, starting transfers between devices, local_step(): lax.all_to_all(flat_grad.reshape(dp_size, part_len), 'dp', 0, 0, tiled=True)  13.3 us
  transfers between devices with their start and end apart: 2, of which 2 were waited for; matrix products, arithmetic and copies ran while one was open for 1% of the time, Pallas kernels for 0%

commit v1 on v0

v1 whole, which is shorter than its diff:
```python
import jax
import jax.numpy as jnp
from jax import lax
from jax.experimental import pallas as pl
from jax.experimental.pallas import tpu as pltpu
from jax.sharding import PartitionSpec as P

STEP = 20
BETA_ONE = 0.9
BETA_TWO = 0.95
ADAM_EPS = 1e-8
DECAY = 0.1
LEARN_RATE = 1e-4
MAX_NORM = 1.0
NORM_EPS = 1e-6
BIAS_ONE = 1.0 - BETA_ONE ** STEP
BIAS_TWO = 1.0 - BETA_TWO ** STEP
ARG_SPECS = (P("dp", None, "tp", None, None), P("dp", "tp", None), P("dp", None, "tp"), P("dp", "tp", None), P("dp", None, None), P("tp", "dp"), P("tp", "dp"), P("tp", "dp"))
OUT_SPECS = (P(None, "tp", None, None), P("tp", None), P(None, "tp"), P("tp", None), P(None, None), P("tp", "dp"), P("tp", "dp"), P("tp", "dp"), P())

MESH = pl.DeviceIdType.MESH
F32 = jnp.float32
BF16 = jnp.bfloat16
LANES = 128
NZ, NY, NC, NX = 8, 4, 2, 4
NK = NY * NC
FLAT = 1051648
MAT = 1048576
PART = FLAT // (NZ * NK)
ROWS = FLAT // LANES
ZROWS = ROWS // NZ
PROWS, QROWS = 96, 48
WIN = PROWS + QROWS
FLATBUF = 8232
FULL = PART // LANES
REST = PART - FULL * LANES
PARTROWS = 136
QKV_ROWS, OUT_ROWS, UP_ROWS, DOWN_ROWS = 3072, 1024, 2048, 2048
OUT_AT = QKV_ROWS
UP_AT = OUT_AT + OUT_ROWS
DOWN_AT = UP_AT + UP_ROWS
NORM_AT = DOWN_AT + DOWN_ROWS


def window_row(k):
    return (k * ZROWS) // NK


def window_lane(k):
    return (k * (ZROWS * LANES // NK)) % LANES


def exchange_kernel(
    g_qkv, g_out, g_up, g_down, g_norms, master, mom_one, mom_two,
    gath_p, gath_q, master_new, m_new, v_new, norm_out,
    in_qkv, in_out, in_up, in_down, in_norms, st_master, st_one, st_two,
    rows_master, rows_one, rows_two, flat,
    send_p, recv_p, send_q, recv_q, sum_p, sum_p_in, sum_q, sum_q_in, win,
    sq_k, sq_z, sq_x,
    in_sem, p_send, p_recv, q_send, q_recv, p2_send, p2_recv, q2_send, q2_recv,
    nk_send, nk_recv, nz_send, nz_recv, nx_send, nx_recv,
    ap1_send, ap1_recv, ap2_send, ap2_recv, ap3_send, ap3_recv,
    aq1_send, aq1_recv, aq2_send, aq2_recv, aq3_send, aq3_recv,
):
    tp = lax.axis_index("tp")
    dp = lax.axis_index("dp")
    z, k = dp // NK, dp % NK
    y, c = k // NC, k % NC

    def z_at(d):
        return lax.rem(z + d, NZ)

    def y_at(d):
        return lax.rem(y + d, NY)

    def k_at(d):
        return y_at(d // NC) * NC + lax.rem(c + d % NC, NC)

    def dev(zz, kk):
        return (tp, zz * NK + kk)

    def rdma(src, dst, send, recv, device):
        return pltpu.make_async_remote_copy(src_ref=src, dst_ref=dst, send_sem=send, recv_sem=recv, device_id=device, device_id_type=MESH)

    loads = [
        pltpu.make_async_copy(src, dst, in_sem.at[i])
        for i, (src, dst) in enumerate((
            (g_qkv, in_qkv), (g_down, in_down), (g_up, in_up), (g_out, in_out), (g_norms, in_norms),
            (master, st_master), (mom_one, st_one), (mom_two, st_two)))
    ]
    for load in loads:
        load.start()

    barrier = pltpu.get_barrier_semaphore()
    peers = [dev(z_at(d), k) for d in range(1, NZ)] + [dev(z, k_at(d)) for d in range(1, NK)]
    peers += [(lax.rem(tp + d, NX), dp) for d in range(1, NX)]
    for peer in peers:
        pl.semaphore_signal(barrier, inc=1, device_id=peer, device_id_type=MESH)

    flat[ROWS:FLATBUF, :] = jnp.zeros((FLATBUF - ROWS, LANES), F32)
    loads[0].wait()
    for col in range(6):
        for blk in range(4):
            tile = in_qkv[col * 128:(col + 1) * 128, blk * 128:(blk + 1) * 128].astype(F32)
            flat[pl.ds(blk * 768 + col, 128, stride=6), :] = tile.T

    def spread(ref, start, count):
        def body(i, _):
            tile = ref[pl.ds(pl.multiple_of(i * 16, 16), 16), :].astype(F32)
            for col in range(4):
                flat[pl.ds(start + i * 64 + col, 16, stride=4), :] = tile[:, col * 128:(col + 1) * 128]
            return 0
        lax.fori_loop(0, count // 64, body, 0)

    loads[1].wait()
    spread(in_down, DOWN_AT, DOWN_ROWS)
    loads[2].wait()
    spread(in_up, UP_AT, UP_ROWS)
    loads[3].wait()
    spread(in_out, OUT_AT, OUT_ROWS)
    loads[4].wait()
    tile = in_norms[...].astype(F32)
    for col in range(4):
        flat[pl.ds(NORM_AT + col, 6, stride=4), :] = tile[:, col * 128:(col + 1) * 128]

    def pack(dz, _):
        base = z_at(dz) * ZROWS
        for dk in range(NK):
            start = base + window_row(k_at(dk))
            send_p[dk, dz] = flat[pl.ds(start, PROWS), :].astype(BF16)
            send_q[dz, dk] = flat[pl.ds(start + PROWS, QROWS), :].astype(BF16)
        return 0
    lax.fori_loop(0, NZ, pack, 0)

    pl.semaphore_wait(barrier, len(peers))

    copies_p = [rdma(send_p.at[d], recv_p.at[d], p_send.at[d], p_recv.at[d], dev(z, k_at(d))) for d in range(1, NK)]
    copies_q = [rdma(send_q.at[d], recv_q.at[d], q_send.at[d], q_recv.at[d], dev(z_at(d), k)) for d in range(1, NZ)]
    for order in (3, 2, 4, 1, 5, 0, 6):
        copies_p[order].start()
        copies_q[order].start()

    for i, (state, rows) in enumerate(((st_master, rows_master), (st_one, rows_one), (st_two, rows_two))):
        loads[5 + i].wait()
        rows[FULL:PARTROWS, :] = jnp.zeros((PARTROWS - FULL, LANES), F32)

        def lift(j, _, state=state, rows=rows):
            for u in range(8):
                rows[pl.ds(j * 8 + u, 1), :] = state[:, pl.ds(pl.multiple_of((j * 8 + u) * LANES, LANES), LANES)]
            return 0
        lax.fori_loop(0, FULL // 8, lift, 0)
        rows[FULL:FULL + 1, 0:REST] = state[:, FULL * LANES:PART]

    order = (4, 3, 5, 2, 6, 1, 7)
    for copy in copies_p:
        copy.wait_recv()
    copies_p2 = {d: rdma(sum_p.at[d], sum_p_in.at[d], p2_send.at[d], p2_recv.at[d], dev(z_at(d), k)) for d in order}
    ready = None
    for d in order + (0,):
        total = send_p[0, d].astype(F32)
        for e in range(1, NK):
            total += recv_p[e, d].astype(F32)
        sum_p[d] = total
        if ready is not None:
            copies_p2[ready].start()
        ready = d

    for copy in copies_q:
        copy.wait_recv()
    copies_q2 = {d: rdma(sum_q.at[d], sum_q_in.at[d], q2_send.at[d], q2_recv.at[d], dev(z, k_at(d))) for d in order}
    ready = None
    for d in order + (0,):
        total = send_q[0, d].astype(F32)
        for e in range(1, NZ):
            total += recv_q[e, d].astype(F32)
        sum_q[d] = total
        if ready is not None:
            copies_q2[ready].start()
        ready = d

    for copy in copies_q2.values():
        copy.wait_recv()
    total = sum_q[0]
    for d in range(1, NK):
        total += sum_q_in[d]
    win[PROWS:WIN, :] = total * (1.0 / (NZ * NK))
    for copy in copies_p2.values():
        copy.wait_recv()
    total = sum_p[0]
    for d in range(1, NZ):
        total += sum_p_in[d]
    win[0:PROWS, :] = total * (1.0 / (NZ * NK))

    lane_at = window_lane(k)
    row = lax.broadcasted_iota(jnp.int32, (WIN, LANES), 0)
    lane = lax.broadcasted_iota(jnp.int32, (WIN, LANES), 1)
    entry = row * LANES + lane - lane_at
    counted = (entry >= 0) & (entry < PART) & ((entry + dp * PART < MAT) | (tp == 0))
    grad = win[...]
    squares = jnp.where(counted, grad * grad, 0.0)
    sq_k[k] = jnp.sum(squares.reshape(WIN // 8, 8, LANES), axis=0)
    copies_nk = [rdma(sq_k.at[k], sq_k.at[k], nk_send.at[d], nk_recv.at[d], dev(z, k_at(d))) for d in range(1, NK)]
    for copy in copies_nk:
        copy.start()
    win[...] = pltpu.roll(grad, lax.rem(LANES - lane_at, LANES), axis=1)
    part_lane = lane[0:PARTROWS]
    mean = jnp.where(part_lane < LANES - lane_at, win[0:PARTROWS, :], win[1:PARTROWS + 1, :])
    index = row[0:PARTROWS] * LANES + part_lane
    mean = jnp.where(index < PART, mean, 0.0)
    is_matrix = index + dp * PART < MAT
    old_master = rows_master[...]
    decayed = jnp.where(is_matrix, DECAY * old_master, 0.0)
    for copy in copies_nk:
        copy.wait_recv()
    total = sq_k[0]
    for i in range(1, NK):
        total += sq_k[i]
    sq_z[z] = total
    copies_nz = [rdma(sq_z.at[z], sq_z.at[z], nz_send.at[d], nz_recv.at[d], dev(z_at(d), k)) for d in range(1, NZ)]
    for copy in copies_nz:
        copy.start()
    for copy in copies_nz:
        copy.wait_recv()
    total = sq_z[0]
    for i in range(1, NZ):
        total += sq_z[i]
    sq_x[tp] = total
    copies_nx = [rdma(sq_x.at[tp], sq_x.at[tp], nx_send.at[d], nx_recv.at[d], (lax.rem(tp + d, NX), dp)) for d in range(1, NX)]
    for copy in copies_nx:
        copy.start()
    for copy in copies_nx:
        copy.wait_recv()
    total = sq_x[0]
    for i in range(1, NX):
        total += sq_x[i]
    norm = jnp.sqrt(jnp.sum(jnp.sum(total, axis=1, keepdims=True), axis=0, keepdims=True))
    norm_out[...] = jnp.broadcast_to(norm, (8, LANES))
    clip = jnp.minimum(1.0, MAX_NORM / (norm + NORM_EPS))

    grad = mean * clip
    m = BETA_ONE * rows_one[...] + (1.0 - BETA_ONE) * grad
    v = BETA_TWO * rows_two[...] + (1.0 - BETA_TWO) * grad * grad
    step_dir = (m / BIAS_ONE) / (jnp.sqrt(v / BIAS_TWO) + ADAM_EPS)
    new = old_master - LEARN_RATE * (step_dir + decayed)
    win[8:8 + PARTROWS, :] = pltpu.roll(new, lane_at, axis=1)
    shifted = jnp.where(lane[0:PARTROWS] >= lane_at, win[8:8 + PARTROWS, :], win[7:7 + PARTROWS, :]).astype(BF16)
    gath_p[c, y, z] = shifted[0:PROWS]
    gath_q[c, z, y, 0:PARTROWS - PROWS] = shifted[PROWS:PARTROWS]
    gath_q[c, z, y, PARTROWS - PROWS:QROWS] = jnp.zeros((WIN - PARTROWS, LANES), BF16)

    partner = dev(z, y * NC + 1 - c)

    def forward_p(d):
        src = gath_p.at[c, y, lax.rem(z + NZ - d, NZ)]
        copies = [rdma(src, src, ap2_send.at[d, e], ap2_recv.at[d, e], dev(z, y_at(e) * NC + c)) for e in (1, 3, 2)]
        for copy in copies:
            copy.start()
        return copies

    own_p, own_q = gath_p.at[c, y, z], gath_q.at[c, z, y]
    near = (1, 7, 2, 6, 3, 5, 4)
    ap1 = {d: rdma(own_p, own_p, ap1_send.at[d], ap1_recv.at[d], dev(z_at(d), k)) for d in near}
    aq1 = {d: rdma(own_q, own_q, aq1_send.at[d], aq1_recv.at[d], dev(z, y_at(d) * NC + c)) for d in (1, 3, 2)}
    for copy in aq1.values():
        copy.start()
    for copy in ap1.values():
        copy.start()
    ap2 = forward_p(0)
    master_new[...] = new
    m_new[...] = m
    v_new[...] = v
    for copy in aq1.values():
        copy.wait_recv()
    q_slab = gath_q.at[c, z]
    aq2 = {d: rdma(q_slab, q_slab, aq2_send.at[d], aq2_recv.at[d], dev(z_at(d), k)) for d in near}
    for copy in aq2.values():
        copy.start()
    aq3 = [rdma(q_slab, q_slab, aq3_send.at[0], aq3_recv.at[0], partner)]
    aq3[0].start()
    for d in near:
        ap1[d].wait_recv()
        ap2 += forward_p(d)
    p_slab = gath_p.at[c, y]
    ap3 = [rdma(p_slab, p_slab, ap3_send.at[0], ap3_recv.at[0], partner)]
    ap3[0].start()
    for d in near:
        aq2[d].wait_recv()
        slab = gath_q.at[c, lax.rem(z + NZ - d, NZ)]
        aq3.append(rdma(slab, slab, aq3_send.at[d], aq3_recv.at[d], partner))
        aq3[-1].start()
    for i, e in enumerate((1, 3, 2)):
        for d in range(NZ):
            ap2[d * 3 + i].wait_recv()
        slab = gath_p.at[c, lax.rem(y + NY - e, NY)]
        ap3.append(rdma(slab, slab, ap3_send.at[e], ap3_recv.at[e], partner))
        ap3[-1].start()
    for copy in aq3 + ap3:
        copy.wait_recv()
    sent = copies_p + copies_q + list(copies_p2.values()) + list(copies_q2.values()) + copies_nk + copies_nz + copies_nx
    sent += list(ap1.values()) + list(aq1.values()) + ap2 + list(aq2.values()) + aq3 + ap3
    for copy in sent:
        copy.wait_send()


def split_kernel(
    gath_p, gath_q, master_rows, m_rows, v_rows,
    p_qkv, p_out, p_up, p_down, p_norms, master_new, m_new, v_new, flat,
):
    for rows, out in ((master_rows, master_new), (m_rows, m_new), (v_rows, v_new)):
        def drop(j, _, rows=rows, out=out):
            for u in range(8):
                out[:, pl.ds(pl.multiple_of((j * 8 + u) * LANES, LANES), LANES)] = rows[pl.ds(j * 8 + u, 1), :]
            return 0
        lax.fori_loop(0, FULL // 8, drop, 0)
        out[:, FULL * LANES:PART] = rows[FULL:FULL + 1, 0:REST]

    lane = lax.broadcasted_iota(jnp.int32, (8, LANES), 1)
    flat[0:8, :] = jnp.zeros((8, LANES), F32)

    def place(zz, _):
        for k in range(NK):
            yy, cc = k // NC, k % NC
            start = zz * ZROWS + window_row(k)
            block = gath_p[cc, yy, zz].astype(F32)
            if window_lane(k):
                head = jnp.where(lane >= window_lane(k), block[0:8], flat[pl.ds(start, 8), :])
                row = lax.broadcasted_iota(jnp.int32, (8, LANES), 0)
                head = jnp.where(row == 0, head, block[0:8])
                flat[pl.ds(start, 8), :] = head
                flat[pl.ds(start + 8, PROWS - 8), :] = block[8:]
            else:
                flat[pl.ds(start, PROWS), :] = block
            flat[pl.ds(start + PROWS, QROWS), :] = gath_q[cc, zz, yy].astype(F32)
        return 0
    lax.fori_loop(0, NZ, place, 0)

    def collect(ref, start, count):
        def body(i, _):
            for col in range(4):
                tile = flat[pl.ds(start + i * 64 + col, 16, stride=4), :]
                ref[pl.ds(pl.multiple_of(i * 16, 16), 16), col * 128:(col + 1) * 128] = tile.astype(BF16)
            return 0
        lax.fori_loop(0, count // 64, body, 0)

    collect(p_out, OUT_AT, OUT_ROWS)
    collect(p_up, UP_AT, UP_ROWS)
    collect(p_down, DOWN_AT, DOWN_ROWS)
    for col in range(4):
        p_norms[:, col * 128:(col + 1) * 128] = flat[pl.ds(NORM_AT + col, 6, stride=4), :].astype(BF16)
    for col in range(6):
        for blk in range(4):
            tile = flat[pl.ds(blk * 768 + col, 128, stride=6), :]
            p_qkv[col * 128:(col + 1) * 128, blk * 128:(blk + 1) * 128] = tile.T.astype(BF16)


def solution(mesh):
    vmem = pl.BlockSpec(memory_space=pltpu.VMEM)
    anyspace = pl.BlockSpec(memory_space=pl.ANY)
    dma = pltpu.SemaphoreType.DMA

    def local_step(g_qkv, g_out, g_up, g_down, g_norms, master, mom_one, mom_two):
        qkv_t = g_qkv[0].transpose(1, 2, 3, 0).reshape(768, 512)
        state = jax.ShapeDtypeStruct((PARTROWS, LANES), F32)
        gath_p, gath_q, master_rows, m_rows, v_rows, norm = pl.pallas_call(
            exchange_kernel,
            out_shape=(
                jax.ShapeDtypeStruct((NC, NY, NZ, PROWS, LANES), BF16),
                jax.ShapeDtypeStruct((NC, NZ, NY, QROWS, LANES), BF16),
                state, state, state,
                jax.ShapeDtypeStruct((8, LANES), F32),
            ),
            in_specs=[anyspace] * 8,
            out_specs=(vmem,) * 6,
            scratch_shapes=[
                pltpu.VMEM((768, 512), BF16), pltpu.VMEM((256, 512), BF16), pltpu.VMEM((512, 512), BF16), pltpu.VMEM((512, 512), BF16), pltpu.VMEM((6, 512), BF16),
                pltpu.VMEM((1, PART), F32), pltpu.VMEM((1, PART), F32), pltpu.VMEM((1, PART), F32),
                pltpu.VMEM((PARTROWS, LANES), F32), pltpu.VMEM((PARTROWS, LANES), F32), pltpu.VMEM((PARTROWS, LANES), F32),
                pltpu.VMEM((FLATBUF, LANES), F32),
                pltpu.VMEM((NK, NZ, PROWS, LANES), BF16), pltpu.VMEM((NK, NZ, PROWS, LANES), BF16),
                pltpu.VMEM((NZ, NK, QROWS, LANES), BF16), pltpu.VMEM((NZ, NK, QROWS, LANES), BF16),
                pltpu.VMEM((NZ, PROWS, LANES), F32), pltpu.VMEM((NZ, PROWS, LANES), F32),
                pltpu.VMEM((NK, QROWS, LANES), F32), pltpu.VMEM((NK, QROWS, LANES), F32),
                pltpu.VMEM((WIN, LANES), F32),
                pltpu.VMEM((NK, 8, LANES), F32), pltpu.VMEM((NZ, 8, LANES), F32), pltpu.VMEM((NX, 8, LANES), F32),
                dma((8,)),
                dma((NK,)), dma((NK,)), dma((NZ,)), dma((NZ,)), dma((NZ,)), dma((NZ,)), dma((NK,)), dma((NK,)),
                dma((NK,)), dma((NK,)), dma((NZ,)), dma((NZ,)), dma((NX,)), dma((NX,)),
                dma((NZ,)), dma((NZ,)), dma((NZ, NY)), dma((NZ, NY)), dma((NY,)), dma((NY,)),
                dma((NY,)), dma((NY,)), dma((NZ,)), dma((NZ,)), dma((NZ,)), dma((NZ,)),
            ],
            compiler_params=pltpu.CompilerParams(collective_id=0, has_side_effects=True),
            name="exchange",
        )(qkv_t, g_out[0], g_up[0], g_down[0], g_norms[0], master, mom_one, mom_two)
        row = jax.ShapeDtypeStruct((1, PART), F32)
        p_qkv, p_out, p_up, p_down, p_norms, master_new, m_new, v_new = pl.pallas_call(
            split_kernel,
            out_shape=(
                jax.ShapeDtypeStruct((768, 512), BF16), jax.ShapeDtypeStruct((256, 512), BF16),
                jax.ShapeDtypeStruct((512, 512), BF16), jax.ShapeDtypeStruct((512, 512), BF16),
                jax.ShapeDtypeStruct((6, 512), BF16), row, row, row,
            ),
            in_specs=[vmem] * 5,
            out_specs=(vmem,) * 8,
            scratch_shapes=[pltpu.VMEM((FLATBUF, LANES), F32)],
            name="split",
        )(gath_p, gath_q, master_rows, m_rows, v_rows)
        p_qkv = p_qkv.reshape(4, 3, 64, 512).transpose(3, 0, 1, 2)
        return p_qkv, p_out, p_up, p_down, p_norms, master_new, m_new, v_new, norm[0, 0]

    return jax.shard_map(local_step, mesh=mesh, in_specs=ARG_SPECS, out_specs=OUT_SPECS, check_vma=False)
```

time: 395 us -> 78.2 us (0.20)
  waiting for transfers between devices: 231 us -> 0 us
  blocking collectives: 77.7 us -> 0 us
  Pallas kernels: 0 us -> 76.2 us
  local copies, waits for them, and re-layouts: 31.6 us -> 1.19 us
  other arithmetic: 22.6 us -> 0 us
  between operations: 16.8 us -> 0.65 us
  starting transfers between devices: 13.5 us -> 0 us
    unnamed x2 -> x0, waiting for transfers between devices: 182 us -> none
    psum x1 -> x0, blocking collectives: 77.7 us -> none  [local_step(): grad_norm = jnp.sqrt(lax.psum(local_sq, ('tp', 'dp')))]
    pallas_call x0 -> x2, Pallas kernels: none -> 76.2 us  [the longest x1 71.6 us: local_step(): pl.pallas_call(exchange_kernel, out_shape=(jax.ShapeDtypeStruct((NC, NY,...]
    all_to_all x1 -> x0, waiting for transfers between devices: 48.9 us -> none  [local_step(): lax.all_to_all(flat_grad.reshape(dp_size, part_len), 'dp', 0, 0, tiled=True)]
    unnamed x32 -> x0, local copies, waits for them, and re-layouts: 19.9 us -> none
    all_to_all x1 -> x0, other arithmetic: 13.5 us -> none  [local_step(): lax.all_to_all(flat_grad.reshape(dp_size, part_len), 'dp', 0, 0, tiled=True)]
    all_to_all x1 -> x0, starting transfers between devices: 13.3 us -> none  [local_step(): lax.all_to_all(flat_grad.reshape(dp_size, part_len), 'dp', 0, 0, tiled=True)]
    reduce_sum x2 -> x0, other arithmetic: 7.26 us -> none  [the longest x1 6.63 us: local_step(): grad_mean = jnp.sum(received, axis=0, dtype=jnp.float32) / dp_size]
  transfers between devices with their start and end apart: 2 -> 0, of which waited for: 2 -> 0; matrix products, arithmetic and copies ran while one was open for 1% -> 0% of each run, Pallas kernels for 0% -> 0%
where the time goes in v1:
time: 78.2 us; the launch traced here: 78 us
  Pallas kernels  76.2 us (97%)
  local copies, waits for them, and re-layouts  1.19 us (2%)
    pallas_call x1, Pallas kernels, local_step(): pl.pallas_call(exchange_kernel, out_shape=(jax.ShapeDtypeStruct((NC, NY,...  71.6 us
    pallas_call x1, Pallas kernels, local_step(): pl.pallas_call(split_kernel, out_shape=(jax.ShapeDtypeStruct((768, 512),...  4.56 us

profile of v1, /device:TPU:1, one launch (start us, length us, event | category | flops | bytes accessed | tf_op | source)
XLA Modules:
  0.0 78.0 jit_solution(3648215521152694264)
XLA Ops:
  0.6 71.6 %exchange.1 = (bf16[2,4,8,96,128]{4,3,2,1,0:T(8,128)(2,1)}, bf16[2,8,4,48,128]{4,3,2,1,0:T(8,128)(2,1)}, f32[136,128]{1,0:T(8,128)}, f32[136,128]{1,0:T(8,128)}, f32[136,128]{1,0:T(8,128)}, /*index=5*/f32[8,128]{1,0:T(8,128)}) custom-call(bf16[768,512]{1,0:T(8,128)(2,1)} %bitcast.13, bf16[256,512]{1,0:T(8,128)(2,1)} %bitcast.16, bf16[512,512]{1,0:T(8,128)(2,1)} %bitcast.14, ...), custom_call_target="tpu_custom_call" | custom-call | tf_op jit(solution)/shard_map/exchange/pallas_call | solution.py:364
  72.2 1.2 %slice.3 = f32[1,1]{1,0:T(1,128)} slice(f32[8,128]{1,0:T(8,128)} %get-tuple-element.36), slice={[0:1], [0:1]} | slice | bytes 8 | tf_op jit(solution)/shard_map/slice | solution.py:408
  73.4 4.6 %split.1 = (bf16[768,512]{1,0:T(8,128)(2,1)}, bf16[256,512]{1,0:T(8,128)(2,1)}, bf16[512,512]{1,0:T(8,128)(2,1)}, bf16[512,512]{1,0:T(8,128)(2,1)}, bf16[6,512]{...) custom-call(bf16[2,4,8,96,128]{4,3,2,1,0:T(8,128)(2,1)} %get-tuple-element.23.gath_p, ...), custom_call_target="tpu_custom_call" | custom-call | tf_op jit(solution)/shard_map/split/pallas_call | solution.py:395

commit v2 on v0

v2 whole, which is shorter than its diff:
```python
import jax
import jax.numpy as jnp
from jax import lax
from jax.experimental import pallas as pl
from jax.experimental.pallas import tpu as pltpu
from jax.sharding import PartitionSpec as P

STEP = 20
BETA_ONE = 0.9
BETA_TWO = 0.95
ADAM_EPS = 1e-8
DECAY = 0.1
LEARN_RATE = 1e-4
MAX_NORM = 1.0
NORM_EPS = 1e-6
BIAS_ONE = 1.0 - BETA_ONE ** STEP
BIAS_TWO = 1.0 - BETA_TWO ** STEP
ARG_SPECS = (P("dp", None, "tp", None, None), P("dp", "tp", None), P("dp", None, "tp"), P("dp", "tp", None), P("dp", None, None), P("tp", "dp"), P("tp", "dp"), P("tp", "dp"))
OUT_SPECS = (P(None, "tp", None, None), P("tp", None), P(None, "tp"), P("tp", None), P(None, None), P("tp", "dp"), P("tp", "dp"), P("tp", "dp"), P())

MESH = pl.DeviceIdType.MESH
F32 = jnp.float32
BF16 = jnp.bfloat16
LANES = 128
NZ, NY, NC, NX = 8, 4, 2, 4
NK = NY * NC
NNEAR = NX * NK
FLAT = 1051648
MAT = 1048576
PART = FLAT // (NZ * NK)
ROWS = FLAT // LANES
ZROWS = ROWS // NZ
FULL = PART // LANES
REST = PART - FULL * LANES
WIN = 136
FLATBUF = 8224
PCHUNKS = (40, 40, 16)
QROWS = WIN - sum(PCHUNKS)
GP = 104
GQ = WIN - GP
QKV_ROWS, OUT_ROWS, UP_ROWS, DOWN_ROWS = 3072, 1024, 2048, 2048
OUT_AT = QKV_ROWS
UP_AT = OUT_AT + OUT_ROWS
DOWN_AT = UP_AT + UP_ROWS
NORM_AT = DOWN_AT + DOWN_ROWS
FAR = (4, 3, 5, 2, 6, 1, 7)
NEAR = (1, 7, 2, 6, 3, 5, 4)
KFAR = (4, 5, 2, 6, 3, 7, 1)


def window_row(k):
    return (k * ZROWS) // NK


def window_lane(k):
    return (k * (ZROWS * LANES // NK)) % LANES


def sum_all(terms):
    total = terms[0]
    for term in terms[1:]:
        total = total + term
    return total


def exchange_kernel(names, *refs):
    r = dict(zip(names, refs))
    tp = lax.axis_index("tp")
    dp = lax.axis_index("dp")
    z, k = dp // NK, dp % NK
    y, c = k // NC, k % NC
    flat = r["flat"]

    def z_at(d):
        return lax.rem(z + d, NZ)

    def y_at(d):
        return lax.rem(y + d, NY)

    def k_at(d):
        return y_at(d // NC) * NC + lax.rem(c + d % NC, NC)

    def dev(zz, kk):
        return (tp, zz * NK + kk)

    def near_dev(d):
        return (lax.rem(tp + d // NK, NX), z * NK + k_at(d % NK))

    def rdma(src, dst, sems, index, device):
        return pltpu.make_async_remote_copy(
            src_ref=src, dst_ref=dst, send_sem=r[sems + "_send"].at[index], recv_sem=r[sems + "_recv"].at[index],
            device_id=device, device_id_type=MESH)
    loads = {
        name: pltpu.make_async_copy(r[name], r["in_" + name], r["in_sem"].at[i])
        for i, name in enumerate(("qkv", "down", "up", "out", "norms", "master", "one", "two"))
    }
    for load in loads.values():
        load.start()

    barrier = pltpu.get_barrier_semaphore()
    peers = [dev(z_at(d), k) for d in range(1, NZ)] + [near_dev(d) for d in range(1, NNEAR)]
    for peer in peers:
        pl.semaphore_signal(barrier, inc=1, device_id=peer, device_id_type=MESH)
    flat[ROWS:FLATBUF, :] = jnp.zeros((FLATBUF - ROWS, LANES), F32)
    loads["qkv"].wait()
    for col in range(6):
        for blk in range(4):
            tile = r["in_qkv"][col * 128:(col + 1) * 128, blk * 128:(blk + 1) * 128].astype(F32)
            flat[pl.ds(blk * 768 + col, 128, stride=6), :] = tile.T

    def spread(name, start, count):
        loads[name].wait()
        ref = r["in_" + name]

        def body(i, _):
            tile = ref[pl.ds(pl.multiple_of(i * 16, 16), 16), :].astype(F32)
            for col in range(4):
                flat[pl.ds(start + i * 64 + col, 16, stride=4), :] = tile[:, col * 128:(col + 1) * 128]
            return 0
        lax.fori_loop(0, count // 64, body, 0)
    spread("down", DOWN_AT, DOWN_ROWS)
    spread("up", UP_AT, UP_ROWS)
    spread("out", OUT_AT, OUT_ROWS)
    loads["norms"].wait()
    tile = r["in_norms"][...].astype(F32)
    for col in range(4):
        flat[pl.ds(NORM_AT + col, 6, stride=4), :] = tile[:, col * 128:(col + 1) * 128]

    send_q, recv_q, sum_q, in_q = r["send_q"], r["recv_q"], r["sum_q"], r["in_q"]
    qstart = sum(PCHUNKS)

    def pack_q(dz, _):
        for dk in range(NK):
            start = z_at(dz) * ZROWS + window_row(k_at(dk)) + qstart
            send_q[dz, dk] = flat[pl.ds(start, QROWS), :].astype(BF16)
        return 0
    lax.fori_loop(0, NZ, pack_q, 0)
    pl.semaphore_wait(barrier, len(peers))
    q_one = {d: rdma(send_q.at[d], recv_q.at[d], "q1", d, dev(z_at(d), k)) for d in FAR}
    for copy in q_one.values():
        copy.start()
    p_one = []
    row_at = 0
    for i, rows in enumerate(PCHUNKS):
        send_p = r[f"send_p{i}"]

        def pack_p(dz, _, rows=rows, row_at=row_at, send_p=send_p):
            for dk in range(NK):
                start = z_at(dz) * ZROWS + window_row(k_at(dk)) + row_at
                send_p[dk, dz] = flat[pl.ds(start, rows), :].astype(BF16)
            return 0
        lax.fori_loop(0, NZ, pack_p, 0)
        p_one.append({d: rdma(send_p.at[d], r[f"recv_p{i}"].at[d], f"p1{i}", d, dev(z, k_at(d))) for d in KFAR})
        for copy in p_one[i].values():
            copy.start()
        row_at += rows

    for name in ("master", "one", "two"):
        loads[name].wait()
        state, rows = r["in_" + name], r["rows_" + name]
        rows[FULL:WIN, :] = jnp.zeros((WIN - FULL, LANES), F32)

        def lift(j, _, state=state, rows=rows):
            for u in range(8):
                rows[pl.ds(j * 8 + u, 1), :] = state[:, pl.ds(pl.multiple_of((j * 8 + u) * LANES, LANES), LANES)]
            return 0
        lax.fori_loop(0, FULL // 8, lift, 0)
        rows[FULL:FULL + 1, 0:REST] = state[:, FULL * LANES:PART]

    def second(copies, send, recv, total, landed, sems, order, device):
        for copy in copies.values():
            copy.wait_recv()
        out = {d: rdma(total.at[d], landed.at[d], sems, d, device(d)) for d in order}
        ready = None
        for d in order + (0,):
            total[d] = sum_all([send[0, d].astype(F32)] + [recv[e, d].astype(F32) for e in range(1, 8)])
            if ready is not None:
                out[ready].start()
            ready = d
        return out

    p_two = []

    def second_p(i):
        p_two.append(second(p_one[i], r[f"send_p{i}"], r[f"recv_p{i}"], r[f"sum_p{i}"], r[f"in_p{i}"], f"p2{i}", FAR, lambda d: dev(z_at(d), k)))

    for i in range(len(PCHUNKS) - 1):
        second_p(i)
    q_two = second(q_one, send_q, recv_q, sum_q, in_q, "q2", KFAR, lambda d: dev(z, k_at(d)))
    second_p(len(PCHUNKS) - 1)

    lane_at = window_lane(k)
    win = r["win"]

    def finish(copies, total, landed, start, rows):
        for copy in copies.values():
            copy.wait_recv()
        mean = sum_all([total[0]] + [landed[d] for d in range(1, 8)]) * (1.0 / (NZ * NK))
        win[start:start + rows, :] = mean
        row = lax.broadcasted_iota(jnp.int32, (rows, LANES), 0) + start
        entry = row * LANES + lax.broadcasted_iota(jnp.int32, (rows, LANES), 1) - lane_at
        counted = (entry >= 0) & (entry < PART) & ((entry + dp * PART < MAT) | (tp == 0))
        squares = jnp.where(counted, mean * mean, 0.0)
        return jnp.sum(squares.reshape(rows // 8, 8, LANES), axis=0)

    squares = []
    row_at = 0
    for i, rows in enumerate(PCHUNKS):
        if i == len(PCHUNKS) - 1:
            squares.append(finish(q_two, sum_q, in_q, qstart, QROWS))
        squares.append(finish(p_two[i], r[f"sum_p{i}"], r[f"in_p{i}"], row_at, rows))
        row_at += rows

    sq_near, sq_z = r["sq_near"], r["sq_z"]
    me = tp * NK + k
    sq_near[me] = jnp.sum(sum_all(squares), axis=0, keepdims=True)
    near = {d: rdma(sq_near.at[me], sq_near.at[me], "near", d, near_dev(d)) for d in range(1, NNEAR)}
    for copy in near.values():
        copy.start()
    lane = lax.broadcasted_iota(jnp.int32, (WIN, LANES), 1)
    row = lax.broadcasted_iota(jnp.int32, (WIN, LANES), 0)
    win[0:WIN, :] = pltpu.roll(win[0:WIN, :], lax.rem(LANES - lane_at, LANES), axis=1)
    mean = jnp.where(lane < LANES - lane_at, win[0:WIN, :], win[1:WIN + 1, :])
    index = row * LANES + lane
    mean = jnp.where(index < PART, mean, 0.0)
    is_matrix = index + dp * PART < MAT
    old_master = r["rows_master"][...]
    decayed = jnp.where(is_matrix, DECAY * old_master, 0.0)
    for copy in near.values():
        copy.wait_recv()
    sq_z[z] = sum_all([sq_near[i] for i in range(NNEAR)])
    across = {d: rdma(sq_z.at[z], sq_z.at[z], "across", d, dev(z_at(d), k)) for d in FAR}
    for copy in across.values():
        copy.start()
    for copy in across.values():
        copy.wait_recv()
    norm = jnp.sqrt(jnp.sum(sum_all([sq_z[i] for i in range(NZ)]), axis=1, keepdims=True))
    r["norm"][...] = norm
    clip = jnp.minimum(1.0, MAX_NORM / (norm + NORM_EPS))

    grad = mean * clip
    m = BETA_ONE * r["rows_one"][...] + (1.0 - BETA_ONE) * grad
    v = BETA_TWO * r["rows_two"][...] + (1.0 - BETA_TWO) * grad * grad
    step_dir = (m / BIAS_ONE) / (jnp.sqrt(v / BIAS_TWO) + ADAM_EPS)
    new = old_master - LEARN_RATE * (step_dir + decayed)
    win[8:8 + WIN, :] = pltpu.roll(new, lane_at, axis=1)
    shifted = jnp.where(lane >= lane_at, win[8:8 + WIN, :], win[7:7 + WIN, :]).astype(BF16)
    gath_p, gath_q = r["gath_p"], r["gath_q"]
    gath_p[z, c, y] = shifted[0:GP]
    gath_q[z, c, y] = shifted[GP:WIN]

    partner = dev(z, y * NC + 1 - c)
    to_y = (1, 3, 2)

    def from_z(d):
        return lax.rem(z + NZ - d, NZ)

    def from_y(d):
        return lax.rem(y + NY - d, NY)

    own_p, own_q = gath_p.at[z, c, y], gath_q.at[z, c, y]
    gq1 = {d: rdma(own_q, own_q, "gq1", d, dev(z, y_at(d) * NC + c)) for d in to_y}
    gp1 = {d: rdma(own_p, own_p, "gp1", d, dev(z_at(d), k)) for d in NEAR}
    gp2, gp3, gq3 = {}, {}, {}

    def relay(zd, yd):
        src = gath_p.at[from_z(zd), c, from_y(yd)]
        gp3[zd, yd] = rdma(src, src, "gp3", (zd, yd), partner)
        gp3[zd, yd].start()

    def spread_p(zd):
        src = gath_p.at[from_z(zd), c, y]
        for yd in to_y:
            gp2[zd, yd] = rdma(src, src, "gp2", (zd, yd), dev(z, y_at(yd) * NC + c))
            gp2[zd, yd].start()
        relay(zd, 0)

    for copy in gq1.values():
        copy.start()
    for copy in gp1.values():
        copy.start()
    spread_p(0)
    r["master_new"][...] = new
    r["m_new"][...] = m
    r["v_new"][...] = v
    for zd in NEAR[:2]:
        gp1[zd].wait_recv()
        spread_p(zd)
    for copy in gq1.values():
        copy.wait_recv()
    slab = gath_q.at[z, c]
    gq2 = {d: rdma(slab, slab, "gq2", d, dev(z_at(d), k)) for d in NEAR}
    for copy in gq2.values():
        copy.start()
    gq3[0] = rdma(slab, slab, "gq3", 0, partner)
    gq3[0].start()
    for zd in NEAR[2:]:
        gp1[zd].wait_recv()
        spread_p(zd)
    for zd in (0,) + NEAR[:-1]:
        for yd in to_y:
            gp2[zd, yd].wait_recv()
            relay(zd, yd)
    for zd in NEAR:
        gq2[zd].wait_recv()
        slab = gath_q.at[from_z(zd), c]
        gq3[zd] = rdma(slab, slab, "gq3", zd, partner)
        gq3[zd].start()
    for yd in to_y:
        gp2[NEAR[-1], yd].wait_recv()
        relay(NEAR[-1], yd)
    for copies in (gp3, gq3):
        for copy in copies.values():
            copy.wait_recv()
    for copies in [q_one, q_two, near, across, gq1, gp1, gp2, gp3, gq2, gq3] + p_one + p_two:
        for copy in copies.values():
            copy.wait_send()


def split_kernel(
    gath_p, gath_q, master_rows, m_rows, v_rows, norm_in,
    p_qkv, p_out, p_up, p_down, p_norms, master_new, m_new, v_new, norm_out,
    flat, out_qkv, out_out, out_up, out_down, out_norms, out_master, out_m, out_v, sem,
):
    norm_out[...] = norm_in[...]
    copies = []

    def flush(src, dst):
        copies.append(pltpu.make_async_copy(src, dst, sem.at[len(copies)]))
        copies[-1].start()

    for rows, out, dst in ((master_rows, out_master, master_new), (m_rows, out_m, m_new), (v_rows, out_v, v_new)):
        def drop(j, _, rows=rows, out=out):
            for u in range(8):
                out[:, pl.ds(pl.multiple_of((j * 8 + u) * LANES, LANES), LANES)] = rows[pl.ds(j * 8 + u, 1), :]
            return 0
        lax.fori_loop(0, FULL // 8, drop, 0)
        out[:, FULL * LANES:PART] = rows[FULL:FULL + 1, 0:REST]
        flush(out, dst)

    lane = lax.broadcasted_iota(jnp.int32, (8, LANES), 1)
    row = lax.broadcasted_iota(jnp.int32, (8, LANES), 0)

    def place(zz, _):
        for k in range(NK):
            yy, cc = k // NC, k % NC
            start = zz * ZROWS + window_row(k)
            block = gath_p[zz, cc, yy].astype(F32)
            head = block[0:8]
            if window_lane(k):
                head = jnp.where((row == 0) & (lane < window_lane(k)), flat[pl.ds(start, 8), :], head)
            flat[pl.ds(start, 8), :] = head
            flat[pl.ds(start + 8, GP - 8), :] = block[8:]
            flat[pl.ds(start + GP, GQ), :] = gath_q[zz, cc, yy].astype(F32)
        return 0

    def collect(ref, start, count):
        def body(i, _):
            for col in range(4):
                tile = flat[pl.ds(start + i * 64 + col, 16, stride=4), :]
                ref[pl.ds(pl.multiple_of(i * 16, 16), 16), col * 128:(col + 1) * 128] = tile.astype(BF16)
            return 0
        lax.fori_loop(0, count // 64, body, 0)

    lax.fori_loop(0, 3, place, 0)
    for col in range(6):
        for blk in range(4):
            tile = flat[pl.ds(blk * 768 + col, 128, stride=6), :]
            out_qkv[col * 128:(col + 1) * 128, blk * 128:(blk + 1) * 128] = tile.T.astype(BF16)
    flush(out_qkv, p_qkv)
    lax.fori_loop(3, 6, place, 0)
    collect(out_out, OUT_AT, OUT_ROWS)
    flush(out_out, p_out)
    collect(out_up, UP_AT, UP_ROWS)
    flush(out_up, p_up)
    lax.fori_loop(6, 8, place, 0)
    collect(out_down, DOWN_AT, DOWN_ROWS)
    for col in range(4):
        out_norms[:, col * 128:(col + 1) * 128] = flat[pl.ds(NORM_AT + col, 6, stride=4), :].astype(BF16)
    flush(out_norms, p_norms)
    flush(out_down, p_down)
    for copy in copies:
        copy.wait()


def solution(mesh):
    vmem = pl.BlockSpec(memory_space=pltpu.VMEM)
    hbm = pl.BlockSpec(memory_space=pltpu.HBM)
    dma = pltpu.SemaphoreType.DMA
    v = pltpu.VMEM

    scratch = {
        "in_qkv": v((768, 512), BF16), "in_out": v((256, 512), BF16), "in_up": v((512, 512), BF16),
        "in_down": v((512, 512), BF16), "in_norms": v((6, 512), BF16),
        "in_master": v((1, PART), F32), "in_one": v((1, PART), F32), "in_two": v((1, PART), F32),
        "rows_master": v((WIN, LANES), F32), "rows_one": v((WIN, LANES), F32), "rows_two": v((WIN, LANES), F32),
        "flat": v((FLATBUF, LANES), F32), "win": v((WIN + 8, LANES), F32),
        "send_q": v((NZ, NK, QROWS, LANES), BF16), "recv_q": v((NZ, NK, QROWS, LANES), BF16),
        "sum_q": v((NK, QROWS, LANES), F32), "in_q": v((NK, QROWS, LANES), F32),
        "sq_near": v((NNEAR, 1, LANES), F32), "sq_z": v((NZ, 1, LANES), F32),
        "in_sem": dma((8,)),
    }
    sems = {"q1": (NZ,), "q2": (NK,), "near": (NNEAR,), "across": (NZ,), "gq1": (NY,), "gq2": (NZ,), "gq3": (NZ,), "gp1": (NZ,), "gp2": (NZ, NY), "gp3": (NZ, NY)}
    for i, rows in enumerate(PCHUNKS):
        scratch[f"send_p{i}"] = v((NK, NZ, rows, LANES), BF16)
        scratch[f"recv_p{i}"] = v((NK, NZ, rows, LANES), BF16)
        scratch[f"sum_p{i}"] = v((NZ, rows, LANES), F32)
        scratch[f"in_p{i}"] = v((NZ, rows, LANES), F32)
        sems[f"p1{i}"] = (NK,)
        sems[f"p2{i}"] = (NZ,)
    for name, shape in sems.items():
        scratch[name + "_send"] = dma(shape)
        scratch[name + "_recv"] = dma(shape)
    operands = ("qkv", "out", "up", "down", "norms", "master", "one", "two")
    results = ("gath_p", "gath_q", "master_new", "m_new", "v_new", "norm")
    names = operands + results + tuple(scratch)

    def local_step(g_qkv, g_out, g_up, g_down, g_norms, master, mom_one, mom_two):
        qkv_t = g_qkv[0].transpose(1, 2, 3, 0).reshape(768, 512)
        state = jax.ShapeDtypeStruct((WIN, LANES), F32)
        one = jax.ShapeDtypeStruct((1, 1), F32)
        gathered = pl.pallas_call(
            lambda *refs: exchange_kernel(names, *refs),
            out_shape=(
                jax.ShapeDtypeStruct((NZ, NC, NY, GP, LANES), BF16),
                jax.ShapeDtypeStruct((NZ, NC, NY, GQ, LANES), BF16),
                state, state, state, one,
            ),
            in_specs=[hbm] * 8,
            out_specs=(vmem,) * 6,
            scratch_shapes=list(scratch.values()),
            compiler_params=pltpu.CompilerParams(collective_id=0, has_side_effects=True, vmem_limit_bytes=28 * 2**20),
            name="exchange",
        )(*[pltpu.with_memory_space_constraint(x, pltpu.HBM) for x in (qkv_t, g_out[0], g_up[0], g_down[0], g_norms[0], master, mom_one, mom_two)])
        shapes = [((768, 512), BF16), ((256, 512), BF16), ((512, 512), BF16), ((512, 512), BF16), ((6, 512), BF16)] + [((1, PART), F32)] * 3
        outs = pl.pallas_call(
            split_kernel,
            out_shape=tuple(jax.ShapeDtypeStruct(s, t) for s, t in shapes) + (one,),
            in_specs=[vmem] * 6,
            out_specs=(hbm,) * 8 + (vmem,),
            scratch_shapes=[v((FLATBUF, LANES), F32)] + [v(s, t) for s, t in shapes] + [dma((8,))],
            compiler_params=pltpu.CompilerParams(vmem_limit_bytes=20 * 2**20),
            name="split",
        )(*gathered)
        p_qkv = outs[0].reshape(4, 3, 64, 512).transpose(3, 0, 1, 2)
        return (p_qkv,) + outs[1:8] + (outs[8].reshape(()),)

    return jax.shard_map(local_step, mesh=mesh, in_specs=ARG_SPECS, out_specs=OUT_SPECS, check_vma=False)
```

time: 395 us -> 70.6 us (0.18)
  waiting for transfers between devices: 231 us -> 0 us
  blocking collectives: 77.7 us -> 0 us
  Pallas kernels: 0 us -> 69.8 us
  local copies, waits for them, and re-layouts: 31.6 us -> 0 us
  other arithmetic: 22.6 us -> 0 us
  between operations: 16.8 us -> 0.65 us
  starting transfers between devices: 13.5 us -> 0 us
    unnamed x2 -> x0, waiting for transfers between devices: 182 us -> none
    psum x1 -> x0, blocking collectives: 77.7 us -> none  [local_step(): grad_norm = jnp.sqrt(lax.psum(local_sq, ('tp', 'dp')))]
    pallas_call x0 -> x2, Pallas kernels: none -> 69.8 us  [the longest x1 66 us: local_step(): pl.pallas_call(lambda *refs: exchange_kernel(names, *refs), out_shape=(ja...]
    all_to_all x1 -> x0, waiting for transfers between devices: 48.9 us -> none  [local_step(): lax.all_to_all(flat_grad.reshape(dp_size, part_len), 'dp', 0, 0, tiled=True)]
    unnamed x32 -> x0, local copies, waits for them, and re-layouts: 19.9 us -> none
    all_to_all x1 -> x0, other arithmetic: 13.5 us -> none  [local_step(): lax.all_to_all(flat_grad.reshape(dp_size, part_len), 'dp', 0, 0, tiled=True)]
    all_to_all x1 -> x0, starting transfers between devices: 13.3 us -> none  [local_step(): lax.all_to_all(flat_grad.reshape(dp_size, part_len), 'dp', 0, 0, tiled=True)]
    reduce_sum x2 -> x0, other arithmetic: 7.26 us -> none  [the longest x1 6.63 us: local_step(): grad_mean = jnp.sum(received, axis=0, dtype=jnp.float32) / dp_size]
  transfers between devices with their start and end apart: 2 -> 0, of which waited for: 2 -> 0; matrix products, arithmetic and copies ran while one was open for 1% -> 0% of each run, Pallas kernels for 0% -> 0%
where the time goes in v2:
time: 70.6 us; the launch traced here: 70.4 us
  Pallas kernels  69.8 us (99%)
    pallas_call x1, Pallas kernels, local_step(): pl.pallas_call(lambda *refs: exchange_kernel(names, *refs), out_shape=(ja...  66 us
    pallas_call x1, Pallas kernels, local_step(): pl.pallas_call(split_kernel, out_shape=tuple((jax.ShapeDtypeStruct(s, t)...  3.81 us

profile of v2, /device:TPU:1, one launch (start us, length us, event | category | flops | bytes accessed | tf_op | source)
XLA Modules:
  0.0 70.4 jit_solution(4882156630463114800)
XLA Ops:
  0.6 66.0 %exchange.1 = (bf16[8,2,4,104,128]{4,3,2,1,0:T(8,128)(2,1)S(1)}, bf16[8,2,4,32,128]{4,3,2,1,0:T(8,128)(2,1)S(1)}, f32[136,128]{1,0:T(8,128)S(1)}, f32[136,128]{1...) custom-call(bf16[768,512]{1,0:T(8,128)(2,1)} %bitcast.13, bf16[256,512]{1,0:T(8,128)(2,1)} %bitcast.16, ...), custom_call_target="tpu_custom_call" | custom-call | tf_op jit(solution)/shard_map/exchange/pallas_call | solution.py:422
  66.6 3.8 %split.1 = (bf16[768,512]{1,0:T(8,128)(2,1)}, bf16[256,512]{1,0:T(8,128)(2,1)}, bf16[512,512]{1,0:T(8,128)(2,1)}, bf16[512,512]{1,0:T(8,128)(2,1)}, bf16[6,512]{...) custom-call(bf16[8,2,4,104,128]{4,3,2,1,0:T(8,128)(2,1)S(1)} %get-tuple-elemen, ...), custom_call_target="tpu_custom_call" | custom-call | tf_op jit(solution)/shard_map/split/pallas_call | solution.py:436
